TPU v7x, 256 devices: a whole 4x4x8 slice. The times are simulated.
256 devices in a mesh: band: 4 (over x_lo, core), fft: 64 (over y, z, x_hi).
Axes of the slice: x: 4 (x_hi: 2, x_lo: 2; x = x_hi * 2 + x_lo), y: 4, z: 8, core: 2. Of those that a mesh axis runs over, the one named last changes fastest.
Arguments:
- orbitals: bfloat16 [16, 2, 262144], P('band', None, 'fft'), may hold values from -6 to 6
- sphere_slot: int32 [262144], P('fft'), may hold values from 0 to 24575, as said below
- stick_column: int32 [8192], P('fft'), may hold values from 0 to 36863, as said below
- potential: float32 [192, 192, 192], P('fft'), may hold values from -3 to 3
- subspace: bfloat16 [64, 2, 262144], P('band', None, 'fft'), may hold values from -0.0234375 to 0.0234375
- previous: bfloat16 [16, 2, 262144], P('band', None, 'fft'), may hold values from -6 to 6
Outputs:
- applied: bfloat16 [16, 2, 262144], P('band', None, 'fft')
- intersection: float32 [2, 64, 16], P(None, 'fft', 'band')
Inputs may be any that keep to these rules, and one draw needn't show every extreme that they name: `sphere_slot`: within each aligned block of 4096 entries the values are distinct. `stick_column`: aligned block d of 128 entries holds distinct columns x * 192 + y with d * 3 <= x < (d + 1) * 3.
All inputs are finite; a program needn't handle non-finite values.
Results may differ from a plain program's by a relative error of at most 0.012.
Values may be sent and summed in bfloat16 or wider, within the bound.
No kernel may reach another device: no remote copies, remote signals or barrier semaphores. Data moves between devices by JAX's collectives and lax.ppermute only.
A program may use at most 64 MiB of HBM per device.

v0:
```python
import functools
import math

import jax
import jax.numpy as jnp
import numpy as np
from jax import lax
from jax.experimental import pallas as pl
from jax.experimental.pallas import tpu as pltpu
from jax.sharding import PartitionSpec as P


BF = jnp.bfloat16
F32 = jnp.float32
N = 192
OWN = 64
DEP = N // OWN
STK = 128
W = 256
ROWS = 8 * DEP
EXT = 2
MSG = EXT + ROWS
GRP = 16
CUT = 512
NT = (((1,), (1,)), ((), ()))


def dot(a, b, dims=(((1,), (0,)), ((), ()))):
    return lax.dot_general(a, b, dims, preferred_element_type=F32)


@functools.cache
def tables():
    def trig(rows, cols, scale):
        angle = (np.outer(rows, cols) % N) * (2.0 * math.pi / N)
        return np.cos(angle) * scale, np.sin(angle) * scale

    nat = np.arange(N)
    dealt = (np.arange(DEP)[:, None] + DEP * np.arange(OWN)[None, :]).reshape(-1)

    half = nat[: N // 2]
    even, odd = (
        np.concatenate([part + DEP * (2 * np.arange(OWN // 2) + (part + q) % 2) for part in range(DEP)]) for q in range(2)
    )
    assert not (even % 2).any() and (odd % 2).all()

    def wide(a, rows, cols):
        out = np.zeros((rows, cols))
        out[: a.shape[0], : a.shape[1]] = a
        return out

    def left(rows, cols, scale, sign, width):
        c, s = trig(rows, cols, scale)
        c, s = wide(c, len(rows), width), wide(s * sign, len(rows), width)
        return np.block([[c, -s], [s, c]])

    def right(rows, cols, scale, sign, order, width):
        c, s = trig(rows, cols, scale)
        c, s = wide(c, N, width), wide(s * sign, N, width)
        full = np.block([[c, s], [-s, c]])
        return full if order is None else full[np.ix_(order, order)]

    packed = np.concatenate([np.arange(128), N + np.arange(128), np.arange(128, N), np.arange(N + 128, 2 * N)])
    by_block = np.arange(2 * N).reshape(2, DEP, 64).transpose(1, 0, 2).reshape(-1)
    inv = 1.0 / N
    out = {
        "zf": left(dealt, nat, 1.0, 1.0, N)[:, by_block],
        "yf": right(nat, nat, 1.0, 1.0, packed, N),
        "xe": left(half, even, 1.0, 1.0, N // 2),
        "xo": left(half, odd, 1.0, 1.0, N // 2),
        "ie": left(even, half, inv, -1.0, N // 2),
        "io": left(odd, half, inv, -1.0, N // 2),
        "yi": right(nat, nat, inv, -1.0, packed, N),
        "zi": left(np.concatenate([nat[::2], nat[1::2]]), dealt, inv, -1.0, N),
    }
    return {k: v.astype(np.float32).astype(BF) for k, v in out.items()}


def iota(shape, dim):
    return lax.broadcasted_iota(jnp.int32, shape, dim)


def column_coords(col):
    c = col.astype(F32)
    x = jnp.floor((c + 0.5) * (1.0 / N))
    return x, c - x * N


def fetch(sems, *pairs):
    copies = [pltpu.make_async_copy(src, dst, sems.at[i]) for i, (src, dst) in enumerate(pairs)]
    for copy in copies:
        copy.start()
    return copies


def pack_kernel(
    orb_hbm, slot_hbm, col_hbm, zf_hbm, out_hbm, a_scr, b_scr, m_scr, out_ref, orb_ref, slot_ref, col_ref, zf_ref, sems
):
    copies = fetch(sems, (slot_hbm, slot_ref), (orb_hbm, orb_ref), (col_hbm, col_ref), (zf_hbm, zf_ref))
    npw = slot_ref.shape[1]
    copies[0].wait()
    slot = slot_ref[...]
    low = (slot >> 7) & 63
    high = (slot >> 13) * STK + (slot & (STK - 1))
    half = 1024
    copies[1].wait()
    for i in range(0, npw, half):
        cut = slice(i, i + half)
        a_scr[:, cut] = jnp.where(iota((DEP * STK, half), 0) == high[:, cut], 1.0, 0.0).astype(BF)
        hit = iota((64, half), 0) == low[:, cut]
        for j in range(8):
            row = orb_ref[j // 2, j % 2 : j % 2 + 1, cut].astype(F32)
            b_scr[64 * j : 64 * (j + 1), cut] = jnp.where(hit, row, 0.0).astype(BF)
    grid = dot(a_scr[...], b_scr[...], NT).astype(BF)
    stick = jnp.concatenate(
        [
            jnp.concatenate([grid[STK * h : STK * (h + 1), STK * b : STK * (b + 1)] for h in range(DEP)], axis=1)
            for b in range(4)
        ],
        axis=0,
    )
    copies[2].wait()
    copies[3].wait()
    wave = dot(zf_ref[...], stick, NT)
    x, y = column_coords(col_ref[...])
    xl = x - DEP * jnp.floor((x + 0.5) * (1.0 / DEP))
    ext = jnp.concatenate([xl, y], axis=0)
    for r in range(DEP):
        for j in range(8):
            base = (j % 2) * N + r * OWN
            m_scr[r, pl.ds(j, OWN, stride=8), :] = wave[base : base + OWN, STK * (j // 2) : STK * (j // 2 + 1)]

    copies = []
    for i in range(OWN // GRP):
        parts = []
        for u in range(i * GRP, (i + 1) * GRP):
            parts += [ext] + [m_scr[r, 8 * u : 8 * u + 8] for r in range(DEP)]
        cut = pl.ds(i * GRP * MSG, GRP * MSG)
        out_ref[cut, :] = jnp.concatenate(parts, axis=0).astype(BF)
        copies.append(pltpu.make_async_copy(out_ref.at[cut], out_hbm.at[cut], sems.at[4 + i]))
        copies[-1].start()
    for copy in copies:
        copy.wait()


def plane_kernel(
    in_ref, pot_hbm, *refs
):
    rows = ROWS
    tabs, (out_ref, oh_scr, xl_scr, lo_scr, hi_scr, pot_scr) = refs[:6], refs[6:12]
    copies = fetch(refs[18], *zip(tabs, refs[12:18]), (pot_hbm, pot_scr))
    yf, xe, xo, ie, io, yi = refs[12:18]
    halves = (lo_scr, hi_scr)

    def spot(k, u):
        return (k + u) % 2 * (N // 2) + k * (OWN // 2) + u // 2

    def scatter(i, carry):
        block = in_ref[pl.ds(pl.multiple_of(i * GRP * MSG, 16), GRP * MSG), :].astype(F32)
        for u in range(GRP):
            d = i * GRP + u
            m = block[MSG * u : MSG * (u + 1)]
            xl, y = m[0:1], m[1:2].astype(jnp.int32)
            xl_scr[pl.ds(d, 1), :] = xl
            hot = jnp.where(iota((N, STK), 0) == y, 1.0, 0.0).astype(BF)
            hot = jnp.concatenate([hot, hot[STK:]], axis=0)
            oh_scr[d] = hot
            lhs = jnp.concatenate([jnp.where(xl == k, m[EXT:], 0.0) for k in range(DEP)], axis=0).astype(BF)
            res = dot(lhs, hot, NT)
            for k in range(DEP):
                for r in range(DEP):
                    base = k * rows + r * 8
                    for h in range(2):
                        at = pl.multiple_of((r * N + spot(k, u) + i * (GRP // 2)) * 8, 8)
                        halves[h][pl.ds(at, 8), :] = res[
                            base : base + 8, h * STK : (h + 1) * STK
                        ]
        return carry

    lax.fori_loop(0, OWN // GRP, scatter, 0)
    for copy in copies:
        copy.wait()

    left = iota((N, STK), 1) < STK // 2

    def mixed(one, two):
        return (
            jnp.where(left, one, pltpu.roll(two, STK // 2, 1)),
            jnp.where(left, pltpu.roll(one, STK // 2, 1), two),
        )

    def plane(r, carry):
        at = r * 8 * N
        lined = []
        for b in range(4):
            low = [lo_scr[pl.ds(at + 2 * b + p, N, stride=8), :] for p in range(2)]
            high = [hi_scr[pl.ds(at + 2 * b + p, N, stride=8), :] for p in range(2)]
            lined.append(jnp.concatenate([*low, jnp.where(left, *high)], axis=1).astype(BF))
        ay = jnp.concatenate([dot(jnp.concatenate(lined[c : c + 2], axis=0), yf[...]) for c in (0, 2)], axis=0)
        ay = ay.reshape(4, N, 2 * N)
        blocks = [jnp.concatenate([ay[b, :, :STK], ay[b, :, STK : 2 * STK]], axis=0) for b in range(4)]
        for b in range(0, 4, 2):
            blocks.append(jnp.concatenate(mixed(ay[b, :, 2 * STK :], ay[b + 1, :, 2 * STK :]), axis=0))
        rows = jnp.concatenate(blocks, axis=1).astype(BF)
        fold = N // 2
        one = dot(xe[...], jnp.concatenate([rows[:fold], rows[N : N + fold]], axis=0))
        two = dot(xo[...], jnp.concatenate([rows[fold:N], rows[N + fold :]], axis=0))
        pot = pot_scr[r]
        pot = jnp.concatenate([pot[:, :STK]] * 4 + [pot[:, STK:]] * 4, axis=1)
        near = jnp.concatenate([pot[:fold]] * 2, axis=0)
        far = jnp.concatenate([pot[fold:]] * 2, axis=0)
        near, far = (one + two) * near, (one - two) * far
        one = dot(ie[...], (near + far).astype(BF))
        two = dot(io[...], (near - far).astype(BF))
        bx = jnp.concatenate([one[:fold], two[:fold], one[fold:], two[fold:]], axis=0)
        tails = []
        for b in range(0, 4, 2):
            cut = slice((4 + b // 2) * STK, (5 + b // 2) * STK)
            tails += mixed(bx[:N, cut], bx[N:, cut])
        lined = [
            jnp.concatenate([bx[:N, b * STK : (b + 1) * STK], bx[N:, b * STK : (b + 1) * STK], tails[b]], axis=1)
            for b in range(4)
        ]
        for c in range(0, 4, 2):
            by = dot(jnp.concatenate(lined[c : c + 2], axis=0).astype(BF), yi[...])
            for b in range(2):
                part = by[b * N : (b + 1) * N]
                high = part[:, 2 * STK :]
                for p in range(2):
                    place = pl.ds(at + 2 * (b + c) + p, N, stride=8)
                    lo_scr[place, :] = part[:, p * STK : (p + 1) * STK]
                    hi_scr[place, :] = jnp.where(left, *((high, 0.0) if p == 0 else (0.0, high)))
        return carry

    lax.fori_loop(0, DEP, plane, 0)

    def gather(i, carry):
        parts = []
        for u in range(GRP // 2):
            pair = [2 * u, 2 * u + 1]
            blocks = []
            for d in pair:
                for k in range(DEP):
                    for r in range(DEP):
                        blocks.append(
                            jnp.concatenate(
                                [
                                    half[pl.ds(pl.multiple_of((r * N + spot(k, d) + i * (GRP // 2)) * 8, 8), 8), :]
                                    for half in halves
                                ],
                                axis=1,
                            )
                        )
            lhs = jnp.concatenate(blocks, axis=0).astype(BF)
            res = dot(lhs, jnp.concatenate([oh_scr[i * GRP + d] for d in pair], axis=1))
            for t, d in enumerate(pair):
                xl = xl_scr[pl.ds(i * GRP + d, 1), :]
                took = [
                    res[(t * DEP + k) * rows : (t * DEP + k + 1) * rows, t * STK : (t + 1) * STK] for k in range(DEP)
                ]
                field = jnp.where(xl == 0.0, took[0], jnp.where(xl == 1.0, took[1], took[2]))
                parts += [jnp.zeros((EXT, STK), F32), field]
        out_ref[pl.ds(pl.multiple_of(i * GRP * MSG, 16), GRP * MSG), :] = jnp.concatenate(parts, axis=0).astype(BF)
        return carry

    lax.fori_loop(0, OWN // GRP, gather, 0)


def ready_kernel(
    orb_hbm, slot_hbm, col_hbm, zi_hbm, hot_ref, base_ref, slot_ref, zi_ref, orb_ref, col_ref, sems
):
    copies = fetch(sems, (slot_hbm, slot_ref), (orb_hbm, orb_ref), (col_hbm, col_ref), (zi_hbm, zi_ref))
    for copy in copies:
        copy.wait()
    x, y = column_coords(col_ref[...])
    x = jnp.where(x >= N // 2, x - N, x)
    y = jnp.where(y >= N // 2, y - N, y)
    square = x * x + y * y
    square = jnp.sum(jnp.where(iota((STK, STK), 0) == iota((STK, STK), 1), square, 0.0), axis=1, keepdims=True)

    def step(i, carry):
        cut = pl.ds(pl.multiple_of(i * CUT, CUT), CUT)
        slot = slot_ref[:, cut]
        z, stick = slot >> 7, slot & (STK - 1)
        hot_ref[:, cut] = jnp.where(iota((W, CUT), 0) == (slot & (W - 1)), 1.0, 0.0).astype(BF)
        fz = jnp.where(z >= N // 2, z - N, z).astype(F32)
        flat = jnp.sum(jnp.where(iota((STK, CUT), 0) == stick, square, 0.0), axis=0, keepdims=True)
        kinetic = (fz * fz + flat) * (2.0 / (N * N))
        for b in range(4):
            base_ref[b, :, cut] = kinetic * orb_ref[b, :, cut].astype(F32)
        return carry

    lax.fori_loop(0, hot_ref.shape[1] // CUT, step, 0)


def wave_kernel(in_ref, hot_ref, base_ref, slot_ref, zi_ref, out_ref, sum_ref, m_scr):
    npw = slot_ref.shape[1]

    def unpour(i, total):
        block = in_ref[pl.ds(pl.multiple_of(i * GRP * MSG, 16), GRP * MSG), :].astype(F32)
        for u in range(GRP):
            total = total + block[MSG * u : MSG * u + 1]
            for r in range(DEP):
                row = MSG * u + EXT + 8 * r
                m_scr[r, pl.ds(pl.multiple_of((i * GRP + u) * 8, 8), 8), :] = block[row : row + 8]
        return total

    total = lax.fori_loop(0, OWN // GRP, unpour, jnp.zeros((1, STK), F32))
    total = total[:, 0:8] + total[:, 8:16] + total[:, 16:24]
    sum_ref[...] = jnp.concatenate([total[:, 0:4], total[:, 4:8]], axis=0)
    cols = []
    for b in range(4):
        picks = [m_scr[r, pl.ds(2 * b + p, OWN, stride=8), :] for p in range(2) for r in range(DEP)]
        cols.append(jnp.concatenate(picks, axis=0))
    spectrum = jnp.concatenate(cols, axis=1).astype(BF)
    sticks = dot(zi_ref[...], spectrum).astype(BF)
    fold = N // 2
    sticks = [
        jnp.concatenate(
            [
                jnp.concatenate(
                    [sticks[p * N + q * fold : p * N + (q + 1) * fold, b * STK : (b + 1) * STK] for q in range(2)], axis=1
                )
                for b in range(4)
            ],
            axis=0,
        )
        for p in range(2)
    ]

    def pick(i, carry):
        cut = pl.ds(pl.multiple_of(i * CUT, CUT), CUT)
        hit = iota((fold, CUT), 0) == slot_ref[:, cut] >> 8
        hot = hot_ref[:, cut]
        lines = []
        for p in range(2):
            res = dot(sticks[p], hot)
            lines.append(
                [jnp.sum(jnp.where(hit, res[b * fold : (b + 1) * fold], 0.0), axis=0, keepdims=True) for b in range(4)]
            )
        for b in range(4):
            done = jnp.concatenate([lines[0][b], lines[1][b]], axis=0) + base_ref[b, :, cut]
            out_ref[b, :, cut] = done.astype(BF)
        return carry

    lax.fori_loop(0, npw // CUT, pick, 0, unroll=2)


def overlap_kernel(sub_ref, *refs):
    refs, out_refs = refs[:4], refs[4:]
    sub = sub_ref[...].astype(F32)
    sub = jnp.concatenate([sub[:, 0], sub[:, 1]], axis=1).astype(BF)
    rows = []
    for ref in refs:
        prev = ref[...].astype(F32)
        re, im = prev[:, 0], prev[:, 1]
        rows.append(jnp.concatenate([re, im], axis=1))
        rows.append(jnp.concatenate([im, -re], axis=1))
    res = dot(sub, jnp.concatenate(rows, axis=0).astype(BF), NT)
    top = res.astype(BF).astype(F32)
    mid = (res - top).astype(BF).astype(F32)
    low = res - top - mid
    pad = jnp.zeros((16, STK - 24), F32)
    for k in range(4):
        cut = slice(8 * k, 8 * (k + 1))
        out_refs[k][...] = jnp.concatenate([top[:, cut], mid[:, cut], low[:, cut], pad], axis=1).astype(BF)


def run(kernel, outs, scratch, args, near, room, to=None):
    space = [pltpu.VMEM if n else pltpu.HBM for n in near]
    return pl.pallas_call(
        kernel,
        out_shape=outs,
        in_specs=[pl.BlockSpec(memory_space=m) for m in space],
        **({} if to is None else {"out_specs": pl.BlockSpec(memory_space=to)}),
        scratch_shapes=scratch,
        compiler_params=pltpu.CompilerParams(vmem_limit_bytes=room << 20),
    )(*[pltpu.with_memory_space_constraint(a, m) for a, m in zip(args, space)])


def like(a):
    return pltpu.VMEM(a.shape, a.dtype)


def stage_pack(*args):
    args = (*args, jnp.asarray(tables()["zf"]))
    npw = args[1].shape[1]
    return run(
        pack_kernel,
        pltpu.HBM((OWN * MSG, STK), BF),
        [
            pltpu.VMEM((DEP * STK, npw), BF),
            pltpu.VMEM((512, npw), BF),
            pltpu.VMEM((DEP, OWN * 8, STK), F32),
            pltpu.VMEM((OWN * MSG, STK), BF),
            *map(like, args),
            pltpu.SemaphoreType.DMA((4 + OWN // GRP,)),
        ],
        args,
        (0, 0, 0, 0),
        24,
        pltpu.HBM,
    )


def stage_over(sub, prevs):
    return run(overlap_kernel, [pltpu.VMEM((16, STK), BF)] * 4, [], (sub, *prevs), (1, 1, 1, 1, 1), 8)


def stage_plane(got, pot):
    args = [jnp.asarray(tables()[k]) for k in ("yf", "xe", "xo", "ie", "io", "yi")]
    return run(
        plane_kernel,
        pltpu.VMEM((OWN * MSG, STK), BF),
        [
            pltpu.VMEM((OWN, W, STK), BF),
            pltpu.VMEM((OWN, STK), F32),
            pltpu.VMEM((ROWS * N, STK), F32),
            pltpu.VMEM((ROWS * N, STK), F32),
            like(pot),
            *map(like, args),
            pltpu.SemaphoreType.DMA((7,)),
        ],
        (got, pot, *args),
        (1, 0, 0, 0, 0, 0, 0, 0),
        32,
    )


def stage_ready(orb, slot, col):
    args = (orb, slot, col, jnp.asarray(tables()["zi"]))
    return run(
        ready_kernel,
        [pltpu.VMEM((W, slot.shape[1]), BF), pltpu.VMEM(orb.shape, F32), like(slot), like(args[3])],
        [like(orb), like(col), pltpu.SemaphoreType.DMA((4,))],
        args,
        (0, 0, 0, 0),
        12,
    )


def stage_wave(got, hot, base, slot, zi):
    return run(
        wave_kernel,
        (jax.ShapeDtypeStruct(base.shape, BF), jax.ShapeDtypeStruct((2, 4), F32)),
        [pltpu.VMEM((DEP, OWN * 8, STK), F32)],
        (got, hot, base, slot, zi),
        (1, 1, 1, 1, 1),
        16,
    )


def exchange(tiles):
    return lax.all_to_all(tiles, "fft", 0, 0, tiled=True).reshape(OWN * MSG, STK)


TILES = (OWN, MSG // 2, 2, STK)


def per_device(orbitals, sphere_slot, stick_column, potential, subspace, previous):
    npw = sphere_slot.shape[0]
    slot = sphere_slot.reshape(1, npw)
    col = stick_column.reshape(1, STK)

    def swapped(a, k):
        return lax.ppermute(a, "band", [(g, g ^ k) for g in range(4)])

    across = swapped(previous, 2)
    send = stage_pack(orbitals, slot, col)
    got = exchange(send.reshape(TILES))
    others = [swapped(previous, 1), across, swapped(across, 1)]
    over = stage_over(subspace, [previous, *others])
    mine = [over[0]] + [swapped(over[k], k) for k in (1, 2, 3)]
    prepared = stage_ready(orbitals, slot, col)
    field = stage_plane(got, potential)
    group = lax.axis_index("band")
    for k in (1, 2):
        mine = [jnp.where((group & k) > 0, mine[i ^ k], mine[i]) for i in range(4)]
    sums = jnp.concatenate(mine, axis=0).reshape(OWN, 1, 1, STK)
    head = jnp.pad(sums, ((0, 0), (0, 0), (0, EXT - 1), (0, 0)))
    back = exchange(lax.dynamic_update_slice(field.reshape(TILES), head, (0, 0, 0, 0)))
    applied, total = stage_wave(back, *prepared)
    return applied, total.reshape(2, 1, 4)


def solution(mesh):
    return jax.shard_map(
        per_device,
        mesh=mesh,
        in_specs=(
            P("band", None, "fft"),
            P("fft"),
            P("fft"),
            P("fft", None, None),
            P("band", None, "fft"),
            P("band", None, "fft"),
        ),
        out_specs=(P("band", None, "fft"), P(None, "fft", "band")),
        check_vma=False,
    )
```

profile of v0, /device:TPU:2, one launch (start us, length us, event | category | flops | bytes accessed | tf_op | source)
XLA Modules:
  0.0 75.4 jit_solution(5733633172961495621)
XLA Ops:
  0.6 4.0 %shard_map.149 = bf16[1664,128]{1,0:T(8,128)(2,1)} custom-call(bf16[4,2,4096]{2,1,0:T(2,128)(2,1)} %orb_hbm.3, s32[1,4096]{1,0:T(1,128)} %bitcast.14, s32[1,128]{1,0:T(1,128)} %bitcast.16, bf16[384,384]{1,0:T(8,128)(2,1)} %constant.30.clone.zf_hbm), custom_call_target="tpu_custom_call" | custom-call | tf_op jit(solution)/shard_map/pallas_call | solution.py:371
  4.6 13.7 %all-to-all-start = ((bf16[64,13,2,128]{3,2,1,0:T(2,128)(2,1)}), bf16[64,13,2,128]{3,2,1,0:T(2,128)(2,1)S(1)}, u32[]{:S(2)}, u32[]{:S(2)}) async-start(bf16[64,13,2,128]{3,2,1,0:T(2,128)(2,1)} %bitcast.13), calls=%async_computation | async-start | bytes 851968 | tf_op jit(solution)/shard_map/all_to_all | solution.py:454
  18.3 1.5 %collective-permute-start.1 = (bf16[4,2,4096]{2,1,0:T(2,128)(2,1)}, bf16[4,2,4096]{2,1,0:T(2,128)(2,1)S(1)}, u32[]{:S(2)}, u32[]{:S(2)}) collective-permute-start(bf16[4,2,4096]{2,1,0:T(2,128)(2,1)} %refs_0_.2), channel_id=1, source_target_pairs={{0,128},{64,192},{128,0},{192,64},{1,129},{65,193},{129,1},{193,65... | collective-permute-start | bytes 196616 | tf_op jit(solution)/shard_map/ppermute | solution.py:466
  19.8 0.0 collective-permute-start
  19.8 3.6 %collective-permute-done.1.refs_2_ = bf16[4,2,4096]{2,1,0:T(2,128)(2,1)S(1)} collective-permute-done((bf16[4,2,4096]{2,1,0:T(2,128)(2,1)}, bf16[4,2,4096]{2,1,0:T(2,128)(2,1)S(1)}, u32[]{:S(2)}, u32[]{:S(2)}) %collective-permute-start.1) | collective-permute-done | bytes 65568 | tf_op jit(solution)/shard_map/ppermute | solution.py:466
  23.4 0.0 collective-permute-start.2
  23.4 0.0 collective-permute-done.refs_1_
  23.4 1.2 %collective-permute-done.2.refs_3_ = bf16[4,2,4096]{2,1,0:T(2,128)(2,1)S(1)} collective-permute-done((bf16[4,2,4096]{2,1,0:T(2,128)(2,1)S(1)}, bf16[4,2,4096]{2,1,0:T(2,128)(2,1)S(1)}, u32[]{:S(2)}, u32[]{:S(2)}) %collective-permute-start.2) | collective-permute-done | bytes 65568 | tf_op jit(solution)/shard_map/ppermute | solution.py:466
  24.7 0.0 copy-start
  24.7 0.9 %copy-done = bf16[16,2,4096]{2,1,0:T(2,128)(2,1)S(1)} copy-done((bf16[16,2,4096]{2,1,0:T(2,128)(2,1)S(1)}, bf16[16,2,4096]{2,1,0:T(2,128)(2,1)}, u32[]{:S(2)}) %copy-start) | copy-done | bytes 262168
  25.6 0.0 copy-start.1
  25.6 0.8 %copy-done.1 = bf16[4,2,4096]{2,1,0:T(2,128)(2,1)S(1)} copy-done((bf16[4,2,4096]{2,1,0:T(2,128)(2,1)S(1)}, bf16[4,2,4096]{2,1,0:T(2,128)(2,1)}, u32[]{:S(2)}) %copy-start.1) | copy-done | bytes 65560
  26.5 0.8 %shard_map.151 = (bf16[16,128]{1,0:T(8,128)(2,1)S(1)}, bf16[16,128]{1,0:T(8,128)(2,1)S(1)}, bf16[16,128]{1,0:T(8,128)(2,1)S(1)}, bf16[16,128]{1,0:T(8,128)(2,1)S(1)}) custom-call(bf16[16,2,4096]{2,1,0:T(2,128)(2,1)S(1)} %copy-done, bf16[4,2,4096]{2,1,0:T(2,128)(2,1)S(1)} %copy-done.1, bf16[4,2,4096]{2,1,0:T(2,128)(2,1)S(1)} %collective-permute-done.refs_1_, ...), custom_call_target="tpu_custom_call" | custom-call | tf_op jit(solution)/shard_map/pallas_call | solution.py:371
  27.3 1.2 %collective-permute-start.3 = (bf16[16,128]{1,0:T(8,128)(2,1)S(1)}, bf16[16,128]{1,0:T(8,128)(2,1)S(1)}, u32[]{:S(2)}, u32[]{:S(2)}) collective-permute-start(bf16[16,128]{1,0:T(8,128)(2,1)S(1)} %get-tuple-element.12), channel_id=1, source_target_pairs={{0,192},{64,128},{128,64},{192,0},{1,193},{65,129},{129,65},{193,1... | collective-permute-start | bytes 12296 | tf_op jit(solution)/shard_map/ppermute | solution.py:466
  28.4 0.7 collective-permute-start.4
  29.1 0.1 collective-permute-start.5
  29.2 1.2 %collective-permute-done.3 = bf16[16,128]{1,0:T(8,128)(2,1)S(1)} collective-permute-done((bf16[16,128]{1,0:T(8,128)(2,1)S(1)}, bf16[16,128]{1,0:T(8,128)(2,1)S(1)}, u32[]{:S(2)}, u32[]{:S(2)}) %collective-permute-start.3) | collective-permute-done | bytes 4128 | tf_op jit(solution)/shard_map/ppermute | solution.py:466
  30.4 1.7 %collective-permute-done.4 = bf16[16,128]{1,0:T(8,128)(2,1)S(1)} collective-permute-done((bf16[16,128]{1,0:T(8,128)(2,1)S(1)}, bf16[16,128]{1,0:T(8,128)(2,1)S(1)}, u32[]{:S(2)}, u32[]{:S(2)}) %collective-permute-start.4) | collective-permute-done | bytes 4128 | tf_op jit(solution)/shard_map/ppermute | solution.py:466
  32.1 0.0 collective-permute-done.5
  32.1 3.5 %all-to-all-done = bf16[64,13,2,128]{3,2,1,0:T(2,128)(2,1)S(1)} async-done(((bf16[64,13,2,128]{3,2,1,0:T(2,128)(2,1)}), bf16[64,13,2,128]{3,2,1,0:T(2,128)(2,1)S(1)}, u32[]{:S(2)}, u32[]{:S(2)}) %all-to-all-start) | async-done | bytes 426016 | tf_op jit(solution)/shard_map/all_to_all | solution.py:454
  35.6 10.0 %shard_map.150 = bf16[1664,128]{1,0:T(8,128)(2,1)} custom-call(bf16[1664,128]{1,0:T(8,128)(2,1)S(1)} %bitcast.11, f32[3,192,192]{2,1,0:T(8,128)} %pot_hbm.1, bf16[384,384]{1,0:T(8,128)(2,1)} %constant.32.clone.refs_0_, bf16[192,192]{1,0:T(8,128)(2,1)} %constant.33.clone.refs_1_, bf16[192,192]{1,0:T(8,128)(2,1)} %constant.34.clone.refs_2_, ...), custom_call_target="tpu_custom_call" | custom-call | tf_op jit(solution)/shard_map/pallas_call | solution.py:371
  45.6 0.7 pad_dynamic-update-slice_fusion
  46.2 9.0 %all-to-all-start.1 = ((bf16[64,13,2,128]{3,2,1,0:T(2,128)(2,1)}), bf16[64,13,2,128]{3,2,1,0:T(2,128)(2,1)S(1)}, u32[]{:S(2)}, u32[]{:S(2)}) async-start(bf16[64,13,2,128]{3,2,1,0:T(2,128)(2,1)} %pad_dynamic-update-slice_fusion), calls=%async_computation.1 | async-start | bytes 851968 | tf_op jit(solution)/shard_map/all_to_all | solution.py:454
  55.2 2.0 %shard_map.152 = (bf16[256,4096]{1,0:T(8,128)(2,1)S(1)}, f32[4,2,4096]{2,1,0:T(2,128)S(1)}, s32[1,4096]{1,0:T(1,128)S(1)}, bf16[384,384]{1,0:T(8,128)(2,1)S(1)}) custom-call(bf16[4,2,4096]{2,1,0:T(2,128)(2,1)} %orb_hbm.3, s32[1,4096]{1,0:T(1,128)} %bitcast.15, s32[1,128]{1,0:T(1,128)} %bitcast.17, bf16[384,384]{1,0:T(8,128)(2,1)} %constant.31.clone.zi_hbm), custom_call_target="tpu_custom_call" | custom-call | tf_op jit(solution)/shard_map/pallas_call | solution.py:371
  57.2 14.5 %all-to-all-done.1 = bf16[64,13,2,128]{3,2,1,0:T(2,128)(2,1)S(1)} async-done(((bf16[64,13,2,128]{3,2,1,0:T(2,128)(2,1)}), bf16[64,13,2,128]{3,2,1,0:T(2,128)(2,1)S(1)}, u32[]{:S(2)}, u32[]{:S(2)}) %all-to-all-start.1) | async-done | bytes 426016 | tf_op jit(solution)/shard_map/all_to_all | solution.py:454
  71.7 3.7 %shard_map.153 = (bf16[4,2,4096]{2,1,0:T(2,128)(2,1)}, f32[2,4]{1,0:T(2,128)}) custom-call(bf16[1664,128]{1,0:T(8,128)(2,1)S(1)} %bitcast.12, bf16[256,4096]{1,0:T(8,128)(2,1)S(1)} %get-tuple-element.16.hot_ref, f32[4,2,4096]{2,1,0:T(2,128)S(1)} %get-tuple-element.17.base_ref, s32[1,4096]{1,0:T(1,128)S(1)} %get-tuple-element.18.slot_ref, ...), custom_call_target="tpu_custom_call" | custom-call | tf_op jit(solution)/shard_map/pallas_call | solution.py:371
  (3 shorter events, 0.0 us)
Async XLA Ops:
  4.6 30.9 %all-to-all-start = ((bf16[64,13,2,128]{3,2,1,0:T(2,128)(2,1)}), bf16[64,13,2,128]{3,2,1,0:T(2,128)(2,1)S(1)}, u32[]{:S(2)}, u32[]{:S(2)}) async-start(bf16[64,13,2,128]{3,2,1,0:T(2,128)(2,1)} %bitcast.13), calls=%async_computation | async-start | bytes 851968 | tf_op jit(solution)/shard_map/all_to_all | solution.py:454
  18.3 5.1 %collective-permute-start.1 = (bf16[4,2,4096]{2,1,0:T(2,128)(2,1)}, bf16[4,2,4096]{2,1,0:T(2,128)(2,1)S(1)}, u32[]{:S(2)}, u32[]{:S(2)}) collective-permute-start(bf16[4,2,4096]{2,1,0:T(2,128)(2,1)} %refs_0_.2), channel_id=1, source_target_pairs={{0,128},{64,192},{128,0},{192,64},{1,129},{65,193},{129,1},{193,65... | collective-permute-start | bytes 196616 | tf_op jit(solution)/shard_map/ppermute | solution.py:466
  19.8 3.6 %collective-permute-start = (bf16[4,2,4096]{2,1,0:T(2,128)(2,1)}, bf16[4,2,4096]{2,1,0:T(2,128)(2,1)S(1)}, u32[]{:S(2)}, u32[]{:S(2)}) collective-permute-start(bf16[4,2,4096]{2,1,0:T(2,128)(2,1)} %refs_0_.2), channel_id=1, source_target_pairs={{0,64},{64,0},{128,192},{192,128},{1,65},{65,1},{129,193},{193,129... | collective-permute-start | bytes 196616 | tf_op jit(solution)/shard_map/ppermute | solution.py:466
  23.4 1.3 %collective-permute-start.2 = (bf16[4,2,4096]{2,1,0:T(2,128)(2,1)S(1)}, bf16[4,2,4096]{2,1,0:T(2,128)(2,1)S(1)}, u32[]{:S(2)}, u32[]{:S(2)}) collective-permute-start(bf16[4,2,4096]{2,1,0:T(2,128)(2,1)S(1)} %collective-permute-done.1.refs_2_), channel_id=1, source_target_pairs={{0,64},{64,0},{128,192},{192,128},{1,65},{65,1},{129,193},{193,129... | collective-permute-start | bytes 196616 | tf_op jit(solution)/shard_map/ppermute | solution.py:466
  24.7 1.0 %copy-start = (bf16[16,2,4096]{2,1,0:T(2,128)(2,1)S(1)}, bf16[16,2,4096]{2,1,0:T(2,128)(2,1)}, u32[]{:S(2)}) copy-start(bf16[16,2,4096]{2,1,0:T(2,128)(2,1)} %sub_ref.1) | copy-start | bytes 786436
  25.6 0.8 %copy-start.1 = (bf16[4,2,4096]{2,1,0:T(2,128)(2,1)S(1)}, bf16[4,2,4096]{2,1,0:T(2,128)(2,1)}, u32[]{:S(2)}) copy-start(bf16[4,2,4096]{2,1,0:T(2,128)(2,1)} %refs_0_.2) | copy-start | bytes 196612
  27.3 3.1 %collective-permute-start.3 = (bf16[16,128]{1,0:T(8,128)(2,1)S(1)}, bf16[16,128]{1,0:T(8,128)(2,1)S(1)}, u32[]{:S(2)}, u32[]{:S(2)}) collective-permute-start(bf16[16,128]{1,0:T(8,128)(2,1)S(1)} %get-tuple-element.12), channel_id=1, source_target_pairs={{0,192},{64,128},{128,64},{192,0},{1,193},{65,129},{129,65},{193,1... | collective-permute-start | bytes 12296 | tf_op jit(solution)/shard_map/ppermute | solution.py:466
  28.4 3.6 %collective-permute-start.4 = (bf16[16,128]{1,0:T(8,128)(2,1)S(1)}, bf16[16,128]{1,0:T(8,128)(2,1)S(1)}, u32[]{:S(2)}, u32[]{:S(2)}) collective-permute-start(bf16[16,128]{1,0:T(8,128)(2,1)S(1)} %get-tuple-element.13), channel_id=1, source_target_pairs={{0,128},{64,192},{128,0},{192,64},{1,129},{65,193},{129,1},{193,65... | collective-permute-start | bytes 12296 | tf_op jit(solution)/shard_map/ppermute | solution.py:466
  29.1 2.9 %collective-permute-start.5 = (bf16[16,128]{1,0:T(8,128)(2,1)S(1)}, bf16[16,128]{1,0:T(8,128)(2,1)S(1)}, u32[]{:S(2)}, u32[]{:S(2)}) collective-permute-start(bf16[16,128]{1,0:T(8,128)(2,1)S(1)} %get-tuple-element.14), channel_id=1, source_target_pairs={{0,64},{64,0},{128,192},{192,128},{1,65},{65,1},{129,193},{193,129... | collective-permute-start | bytes 12296 | tf_op jit(solution)/shard_map/ppermute | solution.py:466
  46.2 25.5 %all-to-all-start.1 = ((bf16[64,13,2,128]{3,2,1,0:T(2,128)(2,1)}), bf16[64,13,2,128]{3,2,1,0:T(2,128)(2,1)S(1)}, u32[]{:S(2)}, u32[]{:S(2)}) async-start(bf16[64,13,2,128]{3,2,1,0:T(2,128)(2,1)} %pad_dynamic-update-slice_fusion), calls=%async_computation.1 | async-start | bytes 851968 | tf_op jit(solution)/shard_map/all_to_all | solution.py:454
where the time goes:
time: 76.4 us; the launch traced here: 75.4 us
  starting transfers between devices  26.1 us (34%)
  waiting for transfers between devices  25.7 us (34%)
  Pallas kernels  20.5 us (27%)
  local copies, waits for them, and re-layouts  2.47 us (3%)
    all_to_all x2, starting transfers between devices, exchange(): lax.all_to_all(tiles, 'fft', 0, 0, tiled=True).reshape(OWN * MSG, STK)  22.6 us
    pallas_call x5, Pallas kernels, run(): pl.pallas_call(kernel, out_shape=outs, in_specs=[pl.BlockSpec(memory_spac...  20.5 us
    all_to_all x2, waiting for transfers between devices, exchange(): lax.all_to_all(tiles, 'fft', 0, 0, tiled=True).reshape(OWN * MSG, STK)  18 us
    ppermute x6, waiting for transfers between devices, swapped(): return lax.ppermute(a, 'band', [(g, g ^ k) for g in range(4)])  7.7 us
    ppermute x6, starting transfers between devices, swapped(): return lax.ppermute(a, 'band', [(g, g ^ k) for g in range(4)])  3.46 us
    unnamed x5, local copies, waits for them, and re-layouts  1.82 us
  transfers between devices with their start and end apart: 8, of which 6 were waited for; matrix products, arithmetic and copies ran while one was open for 0% of the time, Pallas kernels for 4%

commit v1 on v0

--- a/solution.py
+++ b/solution.py
@@ -155,14 +155,16 @@
     def spot(k, u):
         return (k + u) % 2 * (N // 2) + k * (OWN // 2) + u // 2
 
+    rise = iota((N, STK), 0).astype(F32).astype(BF)
+
     def scatter(i, carry):
         block = in_ref[pl.ds(pl.multiple_of(i * GRP * MSG, 16), GRP * MSG), :].astype(F32)
         for u in range(GRP):
             d = i * GRP + u
             m = block[MSG * u : MSG * (u + 1)]
-            xl, y = m[0:1], m[1:2].astype(jnp.int32)
+            xl, y = m[0:1], m[1:2].astype(BF)
             xl_scr[pl.ds(d, 1), :] = xl
-            hot = jnp.where(iota((N, STK), 0) == y, 1.0, 0.0).astype(BF)
+            hot = jnp.where(rise == y, BF(1), BF(0))
             hot = jnp.concatenate([hot, hot[STK:]], axis=0)
             oh_scr[d] = hot
             lhs = jnp.concatenate([jnp.where(xl == k, m[EXT:], 0.0) for k in range(DEP)], axis=0).astype(BF)
@@ -343,7 +345,7 @@
             out_ref[b, :, cut] = done.astype(BF)
         return carry
 
-    lax.fori_loop(0, npw // CUT, pick, 0, unroll=2)
+    lax.fori_loop(0, npw // CUT, pick, 0, unroll=4)
 
 
 def overlap_kernel(sub_ref, *refs):

time: 76.4 us -> 75.6 us (0.990)
  Pallas kernels: 20.5 us -> 19.7 us
    pallas_call x5, Pallas kernels: 20.5 us -> 19.7 us  [run(): pl.pallas_call(kernel, out_shape=outs, in_specs=[pl.BlockSpec(memory_spac...]
where the time goes in v1:
time: 75.6 us; the launch traced here: 74.6 us
  starting transfers between devices  26.1 us (35%)
  waiting for transfers between devices  25.7 us (34%)
  Pallas kernels  19.7 us (26%)
  local copies, waits for them, and re-layouts  2.47 us (3%)
    all_to_all x2, starting transfers between devices, exchange(): lax.all_to_all(tiles, 'fft', 0, 0, tiled=True).reshape(OWN * MSG, STK)  22.7 us
    pallas_call x5, Pallas kernels, run(): pl.pallas_call(kernel, out_shape=outs, in_specs=[pl.BlockSpec(memory_spac...  19.7 us
    all_to_all x2, waiting for transfers between devices, exchange(): lax.all_to_all(tiles, 'fft', 0, 0, tiled=True).reshape(OWN * MSG, STK)  18 us
    ppermute x6, waiting for transfers between devices, swapped(): return lax.ppermute(a, 'band', [(g, g ^ k) for g in range(4)])  7.7 us
    ppermute x6, starting transfers between devices, swapped(): return lax.ppermute(a, 'band', [(g, g ^ k) for g in range(4)])  3.46 us
    unnamed x5, local copies, waits for them, and re-layouts  1.82 us
  transfers between devices with their start and end apart: 8, of which 6 were waited for; matrix products, arithmetic and copies ran while one was open for 0% of the time, Pallas kernels for 4%

profile of v1, /device:TPU:2, one launch (start us, length us, event | category | flops | bytes accessed | tf_op | source)
XLA Modules:
  0.0 74.6 jit_solution(14363626300258986217)
XLA Ops:
  0.6 4.0 %shard_map.149 = bf16[1664,128]{1,0:T(8,128)(2,1)} custom-call(bf16[4,2,4096]{2,1,0:T(2,128)(2,1)} %orb_hbm.3, s32[1,4096]{1,0:T(1,128)} %bitcast.14, s32[1,128]{1,0:T(1,128)} %bitcast.16, bf16[384,384]{1,0:T(8,128)(2,1)} %constant.30.clone.zf_hbm), custom_call_target="tpu_custom_call" | custom-call | tf_op jit(solution)/shard_map/pallas_call | solution.py:373
  4.6 13.7 %all-to-all-start = ((bf16[64,13,2,128]{3,2,1,0:T(2,128)(2,1)}), bf16[64,13,2,128]{3,2,1,0:T(2,128)(2,1)S(1)}, u32[]{:S(2)}, u32[]{:S(2)}) async-start(bf16[64,13,2,128]{3,2,1,0:T(2,128)(2,1)} %bitcast.13), calls=%async_computation | async-start | bytes 851968 | tf_op jit(solution)/shard_map/all_to_all | solution.py:456
  18.3 1.5 %collective-permute-start.1 = (bf16[4,2,4096]{2,1,0:T(2,128)(2,1)}, bf16[4,2,4096]{2,1,0:T(2,128)(2,1)S(1)}, u32[]{:S(2)}, u32[]{:S(2)}) collective-permute-start(bf16[4,2,4096]{2,1,0:T(2,128)(2,1)} %refs_0_.2), channel_id=1, source_target_pairs={{0,128},{64,192},{128,0},{192,64},{1,129},{65,193},{129,1},{193,65... | collective-permute-start | bytes 196616 | tf_op jit(solution)/shard_map/ppermute | solution.py:468
  19.8 0.0 collective-permute-start
  19.8 3.6 %collective-permute-done.1.refs_2_ = bf16[4,2,4096]{2,1,0:T(2,128)(2,1)S(1)} collective-permute-done((bf16[4,2,4096]{2,1,0:T(2,128)(2,1)}, bf16[4,2,4096]{2,1,0:T(2,128)(2,1)S(1)}, u32[]{:S(2)}, u32[]{:S(2)}) %collective-permute-start.1) | collective-permute-done | bytes 65568 | tf_op jit(solution)/shard_map/ppermute | solution.py:468
  23.4 0.0 collective-permute-start.2
  23.4 0.0 collective-permute-done.refs_1_
  23.4 1.2 %collective-permute-done.2.refs_3_ = bf16[4,2,4096]{2,1,0:T(2,128)(2,1)S(1)} collective-permute-done((bf16[4,2,4096]{2,1,0:T(2,128)(2,1)S(1)}, bf16[4,2,4096]{2,1,0:T(2,128)(2,1)S(1)}, u32[]{:S(2)}, u32[]{:S(2)}) %collective-permute-start.2) | collective-permute-done | bytes 65568 | tf_op jit(solution)/shard_map/ppermute | solution.py:468
  24.7 0.0 copy-start
  24.7 0.9 %copy-done = bf16[16,2,4096]{2,1,0:T(2,128)(2,1)S(1)} copy-done((bf16[16,2,4096]{2,1,0:T(2,128)(2,1)S(1)}, bf16[16,2,4096]{2,1,0:T(2,128)(2,1)}, u32[]{:S(2)}) %copy-start) | copy-done | bytes 262168
  25.6 0.0 copy-start.1
  25.6 0.8 %copy-done.1 = bf16[4,2,4096]{2,1,0:T(2,128)(2,1)S(1)} copy-done((bf16[4,2,4096]{2,1,0:T(2,128)(2,1)S(1)}, bf16[4,2,4096]{2,1,0:T(2,128)(2,1)}, u32[]{:S(2)}) %copy-start.1) | copy-done | bytes 65560
  26.5 0.8 %shard_map.151 = (bf16[16,128]{1,0:T(8,128)(2,1)S(1)}, bf16[16,128]{1,0:T(8,128)(2,1)S(1)}, bf16[16,128]{1,0:T(8,128)(2,1)S(1)}, bf16[16,128]{1,0:T(8,128)(2,1)S(1)}) custom-call(bf16[16,2,4096]{2,1,0:T(2,128)(2,1)S(1)} %copy-done, bf16[4,2,4096]{2,1,0:T(2,128)(2,1)S(1)} %copy-done.1, bf16[4,2,4096]{2,1,0:T(2,128)(2,1)S(1)} %collective-permute-done.refs_1_, ...), custom_call_target="tpu_custom_call" | custom-call | tf_op jit(solution)/shard_map/pallas_call | solution.py:373
  27.3 1.2 %collective-permute-start.3 = (bf16[16,128]{1,0:T(8,128)(2,1)S(1)}, bf16[16,128]{1,0:T(8,128)(2,1)S(1)}, u32[]{:S(2)}, u32[]{:S(2)}) collective-permute-start(bf16[16,128]{1,0:T(8,128)(2,1)S(1)} %get-tuple-element.12), channel_id=1, source_target_pairs={{0,192},{64,128},{128,64},{192,0},{1,193},{65,129},{129,65},{193,1... | collective-permute-start | bytes 12296 | tf_op jit(solution)/shard_map/ppermute | solution.py:468
  28.4 0.7 collective-permute-start.4
  29.1 0.1 collective-permute-start.5
  29.2 1.2 %collective-permute-done.3 = bf16[16,128]{1,0:T(8,128)(2,1)S(1)} collective-permute-done((bf16[16,128]{1,0:T(8,128)(2,1)S(1)}, bf16[16,128]{1,0:T(8,128)(2,1)S(1)}, u32[]{:S(2)}, u32[]{:S(2)}) %collective-permute-start.3) | collective-permute-done | bytes 4128 | tf_op jit(solution)/shard_map/ppermute | solution.py:468
  30.4 1.7 %collective-permute-done.4 = bf16[16,128]{1,0:T(8,128)(2,1)S(1)} collective-permute-done((bf16[16,128]{1,0:T(8,128)(2,1)S(1)}, bf16[16,128]{1,0:T(8,128)(2,1)S(1)}, u32[]{:S(2)}, u32[]{:S(2)}) %collective-permute-start.4) | collective-permute-done | bytes 4128 | tf_op jit(solution)/shard_map/ppermute | solution.py:468
  32.1 0.0 collective-permute-done.5
  32.1 3.5 %all-to-all-done = bf16[64,13,2,128]{3,2,1,0:T(2,128)(2,1)S(1)} async-done(((bf16[64,13,2,128]{3,2,1,0:T(2,128)(2,1)}), bf16[64,13,2,128]{3,2,1,0:T(2,128)(2,1)S(1)}, u32[]{:S(2)}, u32[]{:S(2)}) %all-to-all-start) | async-done | bytes 426016 | tf_op jit(solution)/shard_map/all_to_all | solution.py:456
  35.6 9.4 %shard_map.150 = bf16[1664,128]{1,0:T(8,128)(2,1)} custom-call(bf16[1664,128]{1,0:T(8,128)(2,1)S(1)} %bitcast.11, f32[3,192,192]{2,1,0:T(8,128)} %pot_hbm.1, bf16[384,384]{1,0:T(8,128)(2,1)} %constant.32.clone.refs_0_, bf16[192,192]{1,0:T(8,128)(2,1)} %constant.33.clone.refs_1_, bf16[192,192]{1,0:T(8,128)(2,1)} %constant.34.clone.refs_2_, ...), custom_call_target="tpu_custom_call" | custom-call | tf_op jit(solution)/shard_map/pallas_call | solution.py:373
  45.0 0.7 pad_dynamic-update-slice_fusion
  45.7 9.0 %all-to-all-start.1 = ((bf16[64,13,2,128]{3,2,1,0:T(2,128)(2,1)}), bf16[64,13,2,128]{3,2,1,0:T(2,128)(2,1)S(1)}, u32[]{:S(2)}, u32[]{:S(2)}) async-start(bf16[64,13,2,128]{3,2,1,0:T(2,128)(2,1)} %pad_dynamic-update-slice_fusion), calls=%async_computation.1 | async-start | bytes 851968 | tf_op jit(solution)/shard_map/all_to_all | solution.py:456
  54.7 2.0 %shard_map.152 = (bf16[256,4096]{1,0:T(8,128)(2,1)S(1)}, f32[4,2,4096]{2,1,0:T(2,128)S(1)}, s32[1,4096]{1,0:T(1,128)S(1)}, bf16[384,384]{1,0:T(8,128)(2,1)S(1)}) custom-call(bf16[4,2,4096]{2,1,0:T(2,128)(2,1)} %orb_hbm.3, s32[1,4096]{1,0:T(1,128)} %bitcast.15, s32[1,128]{1,0:T(1,128)} %bitcast.17, bf16[384,384]{1,0:T(8,128)(2,1)} %constant.31.clone.zi_hbm), custom_call_target="tpu_custom_call" | custom-call | tf_op jit(solution)/shard_map/pallas_call | solution.py:373
  56.7 14.5 %all-to-all-done.1 = bf16[64,13,2,128]{3,2,1,0:T(2,128)(2,1)S(1)} async-done(((bf16[64,13,2,128]{3,2,1,0:T(2,128)(2,1)}), bf16[64,13,2,128]{3,2,1,0:T(2,128)(2,1)S(1)}, u32[]{:S(2)}, u32[]{:S(2)}) %all-to-all-start.1) | async-done | bytes 426016 | tf_op jit(solution)/shard_map/all_to_all | solution.py:456
  71.2 3.4 %shard_map.153 = (bf16[4,2,4096]{2,1,0:T(2,128)(2,1)}, f32[2,4]{1,0:T(2,128)}) custom-call(bf16[1664,128]{1,0:T(8,128)(2,1)S(1)} %bitcast.12, bf16[256,4096]{1,0:T(8,128)(2,1)S(1)} %get-tuple-element.16.hot_ref, f32[4,2,4096]{2,1,0:T(2,128)S(1)} %get-tuple-element.17.base_ref, s32[1,4096]{1,0:T(1,128)S(1)} %get-tuple-element.18.slot_ref, ...), custom_call_target="tpu_custom_call" | custom-call | tf_op jit(solution)/shard_map/pallas_call | solution.py:373
  (3 shorter events, 0.0 us)
Async XLA Ops:
  4.6 30.9 %all-to-all-start = ((bf16[64,13,2,128]{3,2,1,0:T(2,128)(2,1)}), bf16[64,13,2,128]{3,2,1,0:T(2,128)(2,1)S(1)}, u32[]{:S(2)}, u32[]{:S(2)}) async-start(bf16[64,13,2,128]{3,2,1,0:T(2,128)(2,1)} %bitcast.13), calls=%async_computation | async-start | bytes 851968 | tf_op jit(solution)/shard_map/all_to_all | solution.py:456
  18.3 5.1 %collective-permute-start.1 = (bf16[4,2,4096]{2,1,0:T(2,128)(2,1)}, bf16[4,2,4096]{2,1,0:T(2,128)(2,1)S(1)}, u32[]{:S(2)}, u32[]{:S(2)}) collective-permute-start(bf16[4,2,4096]{2,1,0:T(2,128)(2,1)} %refs_0_.2), channel_id=1, source_target_pairs={{0,128},{64,192},{128,0},{192,64},{1,129},{65,193},{129,1},{193,65... | collective-permute-start | bytes 196616 | tf_op jit(solution)/shard_map/ppermute | solution.py:468
  19.8 3.6 %collective-permute-start = (bf16[4,2,4096]{2,1,0:T(2,128)(2,1)}, bf16[4,2,4096]{2,1,0:T(2,128)(2,1)S(1)}, u32[]{:S(2)}, u32[]{:S(2)}) collective-permute-start(bf16[4,2,4096]{2,1,0:T(2,128)(2,1)} %refs_0_.2), channel_id=1, source_target_pairs={{0,64},{64,0},{128,192},{192,128},{1,65},{65,1},{129,193},{193,129... | collective-permute-start | bytes 196616 | tf_op jit(solution)/shard_map/ppermute | solution.py:468
  23.4 1.3 %collective-permute-start.2 = (bf16[4,2,4096]{2,1,0:T(2,128)(2,1)S(1)}, bf16[4,2,4096]{2,1,0:T(2,128)(2,1)S(1)}, u32[]{:S(2)}, u32[]{:S(2)}) collective-permute-start(bf16[4,2,4096]{2,1,0:T(2,128)(2,1)S(1)} %collective-permute-done.1.refs_2_), channel_id=1, source_target_pairs={{0,64},{64,0},{128,192},{192,128},{1,65},{65,1},{129,193},{193,129... | collective-permute-start | bytes 196616 | tf_op jit(solution)/shard_map/ppermute | solution.py:468
  24.7 1.0 %copy-start = (bf16[16,2,4096]{2,1,0:T(2,128)(2,1)S(1)}, bf16[16,2,4096]{2,1,0:T(2,128)(2,1)}, u32[]{:S(2)}) copy-start(bf16[16,2,4096]{2,1,0:T(2,128)(2,1)} %sub_ref.1) | copy-start | bytes 786436
  25.6 0.8 %copy-start.1 = (bf16[4,2,4096]{2,1,0:T(2,128)(2,1)S(1)}, bf16[4,2,4096]{2,1,0:T(2,128)(2,1)}, u32[]{:S(2)}) copy-start(bf16[4,2,4096]{2,1,0:T(2,128)(2,1)} %refs_0_.2) | copy-start | bytes 196612
  27.3 3.1 %collective-permute-start.3 = (bf16[16,128]{1,0:T(8,128)(2,1)S(1)}, bf16[16,128]{1,0:T(8,128)(2,1)S(1)}, u32[]{:S(2)}, u32[]{:S(2)}) collective-permute-start(bf16[16,128]{1,0:T(8,128)(2,1)S(1)} %get-tuple-element.12), channel_id=1, source_target_pairs={{0,192},{64,128},{128,64},{192,0},{1,193},{65,129},{129,65},{193,1... | collective-permute-start | bytes 12296 | tf_op jit(solution)/shard_map/ppermute | solution.py:468
  28.4 3.6 %collective-permute-start.4 = (bf16[16,128]{1,0:T(8,128)(2,1)S(1)}, bf16[16,128]{1,0:T(8,128)(2,1)S(1)}, u32[]{:S(2)}, u32[]{:S(2)}) collective-permute-start(bf16[16,128]{1,0:T(8,128)(2,1)S(1)} %get-tuple-element.13), channel_id=1, source_target_pairs={{0,128},{64,192},{128,0},{192,64},{1,129},{65,193},{129,1},{193,65... | collective-permute-start | bytes 12296 | tf_op jit(solution)/shard_map/ppermute | solution.py:468
  29.1 2.9 %collective-permute-start.5 = (bf16[16,128]{1,0:T(8,128)(2,1)S(1)}, bf16[16,128]{1,0:T(8,128)(2,1)S(1)}, u32[]{:S(2)}, u32[]{:S(2)}) collective-permute-start(bf16[16,128]{1,0:T(8,128)(2,1)S(1)} %get-tuple-element.14), channel_id=1, source_target_pairs={{0,64},{64,0},{128,192},{192,128},{1,65},{65,1},{129,193},{193,129... | collective-permute-start | bytes 12296 | tf_op jit(solution)/shard_map/ppermute | solution.py:468
  45.7 25.6 %all-to-all-start.1 = ((bf16[64,13,2,128]{3,2,1,0:T(2,128)(2,1)}), bf16[64,13,2,128]{3,2,1,0:T(2,128)(2,1)S(1)}, u32[]{:S(2)}, u32[]{:S(2)}) async-start(bf16[64,13,2,128]{3,2,1,0:T(2,128)(2,1)} %pad_dynamic-update-slice_fusion), calls=%async_computation.1 | async-start | bytes 851968 | tf_op jit(solution)/shard_map/all_to_all | solution.py:456

commit v2 on v1

--- a/solution.py
+++ b/solution.py
@@ -101,16 +101,20 @@
     copies[0].wait()
     slot = slot_ref[...]
     low = (slot >> 7) & 63
-    high = (slot >> 13) * STK + (slot & (STK - 1))
+    high = (slot >> 13)
+    stick = slot & (STK - 1)
+    rise = iota((STK, 1024), 0).astype(F32).astype(BF)
     half = 1024
     copies[1].wait()
     for i in range(0, npw, half):
         cut = slice(i, i + half)
-        a_scr[:, cut] = jnp.where(iota((DEP * STK, half), 0) == high[:, cut], 1.0, 0.0).astype(BF)
-        hit = iota((64, half), 0) == low[:, cut]
+        for h in range(DEP):
+            mine = jnp.where(high[:, cut] == h, stick[:, cut], -1).astype(F32).astype(BF)
+            a_scr[STK * h : STK * (h + 1), cut] = jnp.where(rise == mine, BF(1), BF(0))
+        hit = rise[:64] == low[:, cut].astype(F32).astype(BF)
         for j in range(8):
-            row = orb_ref[j // 2, j % 2 : j % 2 + 1, cut].astype(F32)
-            b_scr[64 * j : 64 * (j + 1), cut] = jnp.where(hit, row, 0.0).astype(BF)
+            row = orb_ref[j // 2, j % 2 : j % 2 + 1, cut]
+            b_scr[64 * j : 64 * (j + 1), cut] = jnp.where(hit, row, BF(0))
     grid = dot(a_scr[...], b_scr[...], NT).astype(BF)
     stick = jnp.concatenate(
         [
@@ -234,7 +238,7 @@
                     hi_scr[place, :] = jnp.where(left, *((high, 0.0) if p == 0 else (0.0, high)))
         return carry
 
-    lax.fori_loop(0, DEP, plane, 0)
+    lax.fori_loop(0, DEP, plane, 0, unroll=True)
 
     def gather(i, carry):
         parts = []
@@ -265,7 +269,7 @@
         out_ref[pl.ds(pl.multiple_of(i * GRP * MSG, 16), GRP * MSG), :] = jnp.concatenate(parts, axis=0).astype(BF)
         return carry
 
-    lax.fori_loop(0, OWN // GRP, gather, 0)
+    lax.fori_loop(0, OWN // GRP, gather, 0, unroll=True)
 
 
 def ready_kernel(
@@ -345,7 +349,7 @@
             out_ref[b, :, cut] = done.astype(BF)
         return carry
 
-    lax.fori_loop(0, npw // CUT, pick, 0, unroll=4)
+    lax.fori_loop(0, npw // CUT, pick, 0, unroll=8)
 
 
 def overlap_kernel(sub_ref, *refs):

time: 75.6 us -> 74.3 us (0.983)
  Pallas kernels: 19.7 us -> 18.4 us
    pallas_call x5, Pallas kernels: 19.7 us -> 18.4 us  [run(): pl.pallas_call(kernel, out_shape=outs, in_specs=[pl.BlockSpec(memory_spac...]
where the time goes in v2:
time: 74.3 us; the launch traced here: 73.3 us
  starting transfers between devices  26.1 us (35%)
  waiting for transfers between devices  25.6 us (34%)
  Pallas kernels  18.4 us (25%)
  local copies, waits for them, and re-layouts  2.47 us (3%)
    all_to_all x2, starting transfers between devices, exchange(): lax.all_to_all(tiles, 'fft', 0, 0, tiled=True).reshape(OWN * MSG, STK)  22.6 us
    pallas_call x5, Pallas kernels, run(): pl.pallas_call(kernel, out_shape=outs, in_specs=[pl.BlockSpec(memory_spac...  18.4 us
    all_to_all x2, waiting for transfers between devices, exchange(): lax.all_to_all(tiles, 'fft', 0, 0, tiled=True).reshape(OWN * MSG, STK)  17.9 us
    ppermute x6, waiting for transfers between devices, swapped(): return lax.ppermute(a, 'band', [(g, g ^ k) for g in range(4)])  7.7 us
    ppermute x6, starting transfers between devices, swapped(): return lax.ppermute(a, 'band', [(g, g ^ k) for g in range(4)])  3.47 us
    unnamed x5, local copies, waits for them, and re-layouts  1.82 us
  transfers between devices with their start and end apart: 8, of which 6 were waited for; matrix products, arithmetic and copies ran while one was open for 0% of the time, Pallas kernels for 4%

profile of v2, /device:TPU:2, one launch (start us, length us, event | category | flops | bytes accessed | tf_op | source)
XLA Modules:
  0.0 73.3 jit_solution(7737078512440489007)
XLA Ops:
  0.6 4.0 %shard_map.149 = bf16[1664,128]{1,0:T(8,128)(2,1)} custom-call(bf16[4,2,4096]{2,1,0:T(2,128)(2,1)} %orb_hbm.3, s32[1,4096]{1,0:T(1,128)} %bitcast.14, s32[1,128]{1,0:T(1,128)} %bitcast.16, bf16[384,384]{1,0:T(8,128)(2,1)} %constant.30.clone.zf_hbm), custom_call_target="tpu_custom_call" | custom-call | tf_op jit(solution)/shard_map/pallas_call | solution.py:377
  4.6 13.7 %all-to-all-start = ((bf16[64,13,2,128]{3,2,1,0:T(2,128)(2,1)}), bf16[64,13,2,128]{3,2,1,0:T(2,128)(2,1)S(1)}, u32[]{:S(2)}, u32[]{:S(2)}) async-start(bf16[64,13,2,128]{3,2,1,0:T(2,128)(2,1)} %bitcast.13), calls=%async_computation | async-start | bytes 851968 | tf_op jit(solution)/shard_map/all_to_all | solution.py:460
  18.3 1.5 %collective-permute-start.1 = (bf16[4,2,4096]{2,1,0:T(2,128)(2,1)}, bf16[4,2,4096]{2,1,0:T(2,128)(2,1)S(1)}, u32[]{:S(2)}, u32[]{:S(2)}) collective-permute-start(bf16[4,2,4096]{2,1,0:T(2,128)(2,1)} %refs_0_.2), channel_id=1, source_target_pairs={{0,128},{64,192},{128,0},{192,64},{1,129},{65,193},{129,1},{193,65... | collective-permute-start | bytes 196616 | tf_op jit(solution)/shard_map/ppermute | solution.py:472
  19.8 0.0 collective-permute-start
  19.8 3.6 %collective-permute-done.1.refs_2_ = bf16[4,2,4096]{2,1,0:T(2,128)(2,1)S(1)} collective-permute-done((bf16[4,2,4096]{2,1,0:T(2,128)(2,1)}, bf16[4,2,4096]{2,1,0:T(2,128)(2,1)S(1)}, u32[]{:S(2)}, u32[]{:S(2)}) %collective-permute-start.1) | collective-permute-done | bytes 65568 | tf_op jit(solution)/shard_map/ppermute | solution.py:472
  23.4 0.0 collective-permute-start.2
  23.4 0.0 collective-permute-done.refs_1_
  23.4 1.2 %collective-permute-done.2.refs_3_ = bf16[4,2,4096]{2,1,0:T(2,128)(2,1)S(1)} collective-permute-done((bf16[4,2,4096]{2,1,0:T(2,128)(2,1)S(1)}, bf16[4,2,4096]{2,1,0:T(2,128)(2,1)S(1)}, u32[]{:S(2)}, u32[]{:S(2)}) %collective-permute-start.2) | collective-permute-done | bytes 65568 | tf_op jit(solution)/shard_map/ppermute | solution.py:472
  24.7 0.0 copy-start
  24.7 0.9 %copy-done = bf16[16,2,4096]{2,1,0:T(2,128)(2,1)S(1)} copy-done((bf16[16,2,4096]{2,1,0:T(2,128)(2,1)S(1)}, bf16[16,2,4096]{2,1,0:T(2,128)(2,1)}, u32[]{:S(2)}) %copy-start) | copy-done | bytes 262168
  25.6 0.0 copy-start.1
  25.6 0.8 %copy-done.1 = bf16[4,2,4096]{2,1,0:T(2,128)(2,1)S(1)} copy-done((bf16[4,2,4096]{2,1,0:T(2,128)(2,1)S(1)}, bf16[4,2,4096]{2,1,0:T(2,128)(2,1)}, u32[]{:S(2)}) %copy-start.1) | copy-done | bytes 65560
  26.5 0.8 %shard_map.151 = (bf16[16,128]{1,0:T(8,128)(2,1)S(1)}, bf16[16,128]{1,0:T(8,128)(2,1)S(1)}, bf16[16,128]{1,0:T(8,128)(2,1)S(1)}, bf16[16,128]{1,0:T(8,128)(2,1)S(1)}) custom-call(bf16[16,2,4096]{2,1,0:T(2,128)(2,1)S(1)} %copy-done, bf16[4,2,4096]{2,1,0:T(2,128)(2,1)S(1)} %copy-done.1, bf16[4,2,4096]{2,1,0:T(2,128)(2,1)S(1)} %collective-permute-done.refs_1_, ...), custom_call_target="tpu_custom_call" | custom-call | tf_op jit(solution)/shard_map/pallas_call | solution.py:377
  27.2 1.2 %collective-permute-start.3 = (bf16[16,128]{1,0:T(8,128)(2,1)S(1)}, bf16[16,128]{1,0:T(8,128)(2,1)S(1)}, u32[]{:S(2)}, u32[]{:S(2)}) collective-permute-start(bf16[16,128]{1,0:T(8,128)(2,1)S(1)} %get-tuple-element.12), channel_id=1, source_target_pairs={{0,192},{64,128},{128,64},{192,0},{1,193},{65,129},{129,65},{193,1... | collective-permute-start | bytes 12296 | tf_op jit(solution)/shard_map/ppermute | solution.py:472
  28.4 0.7 collective-permute-start.4
  29.1 0.1 collective-permute-start.5
  29.2 1.2 %collective-permute-done.3 = bf16[16,128]{1,0:T(8,128)(2,1)S(1)} collective-permute-done((bf16[16,128]{1,0:T(8,128)(2,1)S(1)}, bf16[16,128]{1,0:T(8,128)(2,1)S(1)}, u32[]{:S(2)}, u32[]{:S(2)}) %collective-permute-start.3) | collective-permute-done | bytes 4128 | tf_op jit(solution)/shard_map/ppermute | solution.py:472
  30.4 1.7 %collective-permute-done.4 = bf16[16,128]{1,0:T(8,128)(2,1)S(1)} collective-permute-done((bf16[16,128]{1,0:T(8,128)(2,1)S(1)}, bf16[16,128]{1,0:T(8,128)(2,1)S(1)}, u32[]{:S(2)}, u32[]{:S(2)}) %collective-permute-start.4) | collective-permute-done | bytes 4128 | tf_op jit(solution)/shard_map/ppermute | solution.py:472
  32.1 0.0 collective-permute-done.5
  32.1 3.5 %all-to-all-done = bf16[64,13,2,128]{3,2,1,0:T(2,128)(2,1)S(1)} async-done(((bf16[64,13,2,128]{3,2,1,0:T(2,128)(2,1)}), bf16[64,13,2,128]{3,2,1,0:T(2,128)(2,1)S(1)}, u32[]{:S(2)}, u32[]{:S(2)}) %all-to-all-start) | async-done | bytes 426016 | tf_op jit(solution)/shard_map/all_to_all | solution.py:460
  35.6 8.6 %shard_map.150 = bf16[1664,128]{1,0:T(8,128)(2,1)} custom-call(bf16[1664,128]{1,0:T(8,128)(2,1)S(1)} %bitcast.11, f32[3,192,192]{2,1,0:T(8,128)} %pot_hbm.1, bf16[384,384]{1,0:T(8,128)(2,1)} %constant.32.clone.refs_0_, bf16[192,192]{1,0:T(8,128)(2,1)} %constant.33.clone.refs_1_, bf16[192,192]{1,0:T(8,128)(2,1)} %constant.34.clone.refs_2_, ...), custom_call_target="tpu_custom_call" | custom-call | tf_op jit(solution)/shard_map/pallas_call | solution.py:377
  44.1 0.7 pad_dynamic-update-slice_fusion
  44.8 8.9 %all-to-all-start.1 = ((bf16[64,13,2,128]{3,2,1,0:T(2,128)(2,1)}), bf16[64,13,2,128]{3,2,1,0:T(2,128)(2,1)S(1)}, u32[]{:S(2)}, u32[]{:S(2)}) async-start(bf16[64,13,2,128]{3,2,1,0:T(2,128)(2,1)} %pad_dynamic-update-slice_fusion), calls=%async_computation.1 | async-start | bytes 851968 | tf_op jit(solution)/shard_map/all_to_all | solution.py:460
  53.7 2.0 %shard_map.152 = (bf16[256,4096]{1,0:T(8,128)(2,1)S(1)}, f32[4,2,4096]{2,1,0:T(2,128)S(1)}, s32[1,4096]{1,0:T(1,128)S(1)}, bf16[384,384]{1,0:T(8,128)(2,1)S(1)}) custom-call(bf16[4,2,4096]{2,1,0:T(2,128)(2,1)} %orb_hbm.3, s32[1,4096]{1,0:T(1,128)} %bitcast.15, s32[1,128]{1,0:T(1,128)} %bitcast.17, bf16[384,384]{1,0:T(8,128)(2,1)} %constant.31.clone.zi_hbm), custom_call_target="tpu_custom_call" | custom-call | tf_op jit(solution)/shard_map/pallas_call | solution.py:377
  55.8 14.5 %all-to-all-done.1 = bf16[64,13,2,128]{3,2,1,0:T(2,128)(2,1)S(1)} async-done(((bf16[64,13,2,128]{3,2,1,0:T(2,128)(2,1)}), bf16[64,13,2,128]{3,2,1,0:T(2,128)(2,1)S(1)}, u32[]{:S(2)}, u32[]{:S(2)}) %all-to-all-start.1) | async-done | bytes 426016 | tf_op jit(solution)/shard_map/all_to_all | solution.py:460
  70.3 3.1 %shard_map.153 = (bf16[4,2,4096]{2,1,0:T(2,128)(2,1)}, f32[2,4]{1,0:T(2,128)}) custom-call(bf16[1664,128]{1,0:T(8,128)(2,1)S(1)} %bitcast.12, bf16[256,4096]{1,0:T(8,128)(2,1)S(1)} %get-tuple-element.16.hot_ref, f32[4,2,4096]{2,1,0:T(2,128)S(1)} %get-tuple-element.17.base_ref, s32[1,4096]{1,0:T(1,128)S(1)} %get-tuple-element.18.slot_ref, ...), custom_call_target="tpu_custom_call" | custom-call | tf_op jit(solution)/shard_map/pallas_call | solution.py:377
  (3 shorter events, 0.0 us)
Async XLA Ops:
  4.6 30.9 %all-to-all-start = ((bf16[64,13,2,128]{3,2,1,0:T(2,128)(2,1)}), bf16[64,13,2,128]{3,2,1,0:T(2,128)(2,1)S(1)}, u32[]{:S(2)}, u32[]{:S(2)}) async-start(bf16[64,13,2,128]{3,2,1,0:T(2,128)(2,1)} %bitcast.13), calls=%async_computation | async-start | bytes 851968 | tf_op jit(solution)/shard_map/all_to_all | solution.py:460
  18.3 5.1 %collective-permute-start.1 = (bf16[4,2,4096]{2,1,0:T(2,128)(2,1)}, bf16[4,2,4096]{2,1,0:T(2,128)(2,1)S(1)}, u32[]{:S(2)}, u32[]{:S(2)}) collective-permute-start(bf16[4,2,4096]{2,1,0:T(2,128)(2,1)} %refs_0_.2), channel_id=1, source_target_pairs={{0,128},{64,192},{128,0},{192,64},{1,129},{65,193},{129,1},{193,65... | collective-permute-start | bytes 196616 | tf_op jit(solution)/shard_map/ppermute | solution.py:472
  19.8 3.6 %collective-permute-start = (bf16[4,2,4096]{2,1,0:T(2,128)(2,1)}, bf16[4,2,4096]{2,1,0:T(2,128)(2,1)S(1)}, u32[]{:S(2)}, u32[]{:S(2)}) collective-permute-start(bf16[4,2,4096]{2,1,0:T(2,128)(2,1)} %refs_0_.2), channel_id=1, source_target_pairs={{0,64},{64,0},{128,192},{192,128},{1,65},{65,1},{129,193},{193,129... | collective-permute-start | bytes 196616 | tf_op jit(solution)/shard_map/ppermute | solution.py:472
  23.4 1.3 %collective-permute-start.2 = (bf16[4,2,4096]{2,1,0:T(2,128)(2,1)S(1)}, bf16[4,2,4096]{2,1,0:T(2,128)(2,1)S(1)}, u32[]{:S(2)}, u32[]{:S(2)}) collective-permute-start(bf16[4,2,4096]{2,1,0:T(2,128)(2,1)S(1)} %collective-permute-done.1.refs_2_), channel_id=1, source_target_pairs={{0,64},{64,0},{128,192},{192,128},{1,65},{65,1},{129,193},{193,129... | collective-permute-start | bytes 196616 | tf_op jit(solution)/shard_map/ppermute | solution.py:472
  24.7 1.0 %copy-start = (bf16[16,2,4096]{2,1,0:T(2,128)(2,1)S(1)}, bf16[16,2,4096]{2,1,0:T(2,128)(2,1)}, u32[]{:S(2)}) copy-start(bf16[16,2,4096]{2,1,0:T(2,128)(2,1)} %sub_ref.1) | copy-start | bytes 786436
  25.6 0.8 %copy-start.1 = (bf16[4,2,4096]{2,1,0:T(2,128)(2,1)S(1)}, bf16[4,2,4096]{2,1,0:T(2,128)(2,1)}, u32[]{:S(2)}) copy-start(bf16[4,2,4096]{2,1,0:T(2,128)(2,1)} %refs_0_.2) | copy-start | bytes 196612
  27.2 3.1 %collective-permute-start.3 = (bf16[16,128]{1,0:T(8,128)(2,1)S(1)}, bf16[16,128]{1,0:T(8,128)(2,1)S(1)}, u32[]{:S(2)}, u32[]{:S(2)}) collective-permute-start(bf16[16,128]{1,0:T(8,128)(2,1)S(1)} %get-tuple-element.12), channel_id=1, source_target_pairs={{0,192},{64,128},{128,64},{192,0},{1,193},{65,129},{129,65},{193,1... | collective-permute-start | bytes 12296 | tf_op jit(solution)/shard_map/ppermute | solution.py:472
  28.4 3.6 %collective-permute-start.4 = (bf16[16,128]{1,0:T(8,128)(2,1)S(1)}, bf16[16,128]{1,0:T(8,128)(2,1)S(1)}, u32[]{:S(2)}, u32[]{:S(2)}) collective-permute-start(bf16[16,128]{1,0:T(8,128)(2,1)S(1)} %get-tuple-element.13), channel_id=1, source_target_pairs={{0,128},{64,192},{128,0},{192,64},{1,129},{65,193},{129,1},{193,65... | collective-permute-start | bytes 12296 | tf_op jit(solution)/shard_map/ppermute | solution.py:472
  29.1 2.9 %collective-permute-start.5 = (bf16[16,128]{1,0:T(8,128)(2,1)S(1)}, bf16[16,128]{1,0:T(8,128)(2,1)S(1)}, u32[]{:S(2)}, u32[]{:S(2)}) collective-permute-start(bf16[16,128]{1,0:T(8,128)(2,1)S(1)} %get-tuple-element.14), channel_id=1, source_target_pairs={{0,64},{64,0},{128,192},{192,128},{1,65},{65,1},{129,193},{193,129... | collective-permute-start | bytes 12296 | tf_op jit(solution)/shard_map/ppermute | solution.py:472
  44.8 25.5 %all-to-all-start.1 = ((bf16[64,13,2,128]{3,2,1,0:T(2,128)(2,1)}), bf16[64,13,2,128]{3,2,1,0:T(2,128)(2,1)S(1)}, u32[]{:S(2)}, u32[]{:S(2)}) async-start(bf16[64,13,2,128]{3,2,1,0:T(2,128)(2,1)} %pad_dynamic-update-slice_fusion), calls=%async_computation.1 | async-start | bytes 851968 | tf_op jit(solution)/shard_map/all_to_all | solution.py:460
